TPU v7x, 512 devices: a whole 4x8x8 slice. The times are simulated.
512 devices in a mesh: owner: 64 (over z, x, core), rep: 8 (over y).
Axes of the slice: x: 4, y: 8, z: 8, core: 2. Of those that a mesh axis runs over, the one named last changes fastest.
Arguments:
- features: float32 [262144, 256], P(('owner', 'rep')), may hold values from -6 to 6
- group_ids: int32 [262144], P(('owner', 'rep')), may hold values from 0 to 65535, as said below
- survive: int32 [262144], P(('owner', 'rep')), may hold values from 0 to 1
- home_row: int32 [65536], replicated, may hold values from 0 to 65535, as said below
- hot_ids: int32 [256], replicated, may hold values from 0 to 65535, as said below
Outputs:
- group_out: float32 [65536, 256], P(('owner', 'rep'))
- group_count: float32 [65536], P(('owner', 'rep'))
- hot_out: float32 [256, 256], P('rep')
- hot_count: float32 [256], P('rep')
Inputs may be any that keep to these rules, and one draw needn't show every extreme that they name: home_row is a permutation of the groups. hot_ids holds 256 different groups. `group_ids`: among the rows of one device, 128 name hot groups, and at most 16 rows name non-hot groups g whose home_row[g] // 1024 is one and the same owner index; on every device some owners get exactly 16 such rows.
All inputs are finite; a program needn't handle non-finite values.
Results may differ from a plain program's by a relative error of at most 0.00007.
Values sent between devices are 32-bit elements; how exact they have to be, the bound alone decides.
A program may use at most 64 MiB of HBM per device.

v0:
```python
import math
import jax
import jax.numpy as jnp
from jax import lax
from jax.sharding import Mesh
from jax.sharding import PartitionSpec as P

OWNER = ("owner_0", "owner_1", "owner_2")
OWNER_REP = ("owner_0", "owner_1", "owner_2", "rep")


def split_up(shard, dim, devices):
    before, after = (shard.shape[:dim], shard.shape[dim + 1 :])
    return jnp.moveaxis(shard.reshape(*before, devices, -1, *after), dim, 0)


def sent_and_summed(shard, axis, dim):
    devices = lax.axis_size(axis)
    parts = lax.all_to_all(split_up(shard, dim, devices), axis, 0, 0, tiled=True)
    return jnp.sum(parts, axis=0)


def in_one_piece(arrays, axis, dim, along):
    columns = [a.reshape(*a.shape[:along], -1) for a in arrays]
    both = jnp.concatenate(columns, axis=along)
    out, at, done = (sent_and_summed(both, axis, dim), 0, [])
    for a, column in zip(arrays, columns):
        slab = out[..., at : at + column.shape[along]]
        done.append(slab.reshape(*slab.shape[:along], *a.shape[along:]))
        at += column.shape[along]
    return tuple(done)


def one_axis_at_a_time(shard, axes):
    for axis in axes:
        shard = lax.psum(shard, axis)
    return shard


def sent_together(arrays, axis, split_dim, concat_dim, along):
    widths = [math.prod(a.shape[along:]) for a in arrays]
    both = jnp.concatenate(
        [a.reshape(*a.shape[:along], w) for a, w in zip(arrays, widths)], axis=along
    )
    out = lax.all_to_all(both, axis, split_axis=split_dim, concat_axis=concat_dim, tiled=True)
    parts = jnp.split(out, [sum(widths[:k]) for k in range(1, len(widths))], axis=along)
    return tuple((b.reshape(*out.shape[:along], *a.shape[along:]) for a, b in zip(arrays, parts)))


def local(features, group_ids, survive, home_row, hot_ids):
    rows = features.shape[0]
    width = features.shape[1]
    owners = lax.axis_size(OWNER)
    own_groups = home_row.shape[0] // owners
    capacity = 2 * rows // owners
    live = survive == 1
    matches = group_ids[:, None] == hot_ids[None, :]
    is_hot = jnp.any(matches, axis=1)
    hot_table = jnp.where(matches & live[:, None], 1.0, 0.0).astype(jnp.float32)
    hot_part = lax.dot_general(
        hot_table,
        features,
        (((0,), (0,)), ((), ())),
        precision=lax.Precision.HIGHEST,
        preferred_element_type=jnp.float32,
    )
    hot_tally = jnp.sum(hot_table, axis=0)
    part_sum, part_tally = in_one_piece((hot_part, hot_tally), "rep", 0, 1)
    hot_sum, hot_count = (
        one_axis_at_a_time(part_sum, OWNER),
        one_axis_at_a_time(part_tally, OWNER),
    )
    hot_out = hot_sum / jnp.sqrt(1.0 + hot_count)[:, None]
    keep = live & jnp.logical_not(is_hot)
    destination = home_row[group_ids]
    target = destination // own_groups
    local_row = (destination % own_groups).astype(jnp.float32)
    member = (
        (target[:, None] == jnp.arange(owners, dtype=jnp.int32)[None, :]) & keep[:, None]
    ).astype(jnp.int32)
    position = jnp.cumsum(member, axis=0) - 1
    placed = jnp.sum(position * member, axis=1)
    target_safe = jnp.where(keep, target, owners)
    placed_safe = jnp.where(keep, placed, 0)
    bucket = (
        jnp.zeros((owners, capacity, width), jnp.float32)
        .at[target_safe, placed_safe]
        .set(features, mode="drop")
    )
    labels = (
        jnp.full((owners, capacity), -1.0, jnp.float32)
        .at[target_safe, placed_safe]
        .set(local_row, mode="drop")
    )
    arrived, arrived_labels = sent_together((bucket, labels), OWNER, 0, 0, 2)
    total_rows = owners * capacity
    block = min(512, total_rows)
    flat_rows = arrived.reshape(total_rows // block, block, width)
    flat_labels = arrived_labels.astype(jnp.int32).reshape(total_rows // block, block)
    columns = jnp.arange(own_groups, dtype=jnp.int32)

    def add_block(carry, item):
        total, tally = carry
        block_rows, block_labels = item
        onehot = (block_labels[:, None] == columns[None, :]).astype(jnp.float32)
        total = total + lax.dot_general(
            onehot,
            block_rows,
            (((0,), (0,)), ((), ())),
            precision=lax.Precision.HIGHEST,
            preferred_element_type=jnp.float32,
        )
        tally = tally + jnp.sum(onehot, axis=0)
        return ((total, tally), None)

    start_carry = (
        jnp.zeros((own_groups, width), jnp.float32),
        jnp.zeros((own_groups,), jnp.float32),
    )
    (dense, dense_tally), _ = lax.scan(add_block, start_carry, (flat_rows, flat_labels))
    cold_sum, group_count = in_one_piece((dense, dense_tally), "rep", 0, 1)
    group_out = cold_sum / jnp.sqrt(1.0 + group_count)[:, None]
    return (group_out, group_count, hot_out, hot_count)


def solution(mesh):
    split = Mesh(
        mesh.devices.reshape(8, 4, 2, mesh.shape["rep"]), ("owner_0", "owner_1", "owner_2", "rep")
    )
    return jax.shard_map(
        local,
        mesh=split,
        in_specs=(P(OWNER_REP, None), P(OWNER_REP), P(OWNER_REP), P(), P()),
        out_specs=(P(OWNER_REP, None), P(OWNER_REP), P("rep", None), P("rep")),
        check_vma=False,
    )
```

profile of v0, /device:TPU:1, one launch (start us, length us, event | category | flops | bytes accessed | tf_op | source)
XLA Modules:
  0.0 193.5 jit_solution(14835666861502887366)
XLA Ops:
  0.6 0.0 copy-start
  0.6 0.0 copy-start.5
  0.7 0.7 compare_select_fusion.2
  1.4 0.9 compare_reduce_fusion
  2.3 3.1 %gather_fusion = s32[512]{0:T(512)S(1)} fusion(s32[65536]{0:T(1024)S(1)} %copy-done, s32[1024]{0:T(1024)S(1)} %pad_clamp_fusion), kind=kCustom, calls=%fused_computation | custom fusion | bytes 6144 | tf_op jit(solution)/shard_map/gather | solution.py:75
  5.5 0.0 copy-done.5
  5.6 1.2 reduce-window.6
  6.8 0.2 slice_reduce_fusion
  7.0 0.1 fusion.19
  7.2 25.2 %scatter_fusion.1 = f32[64,16]{0,1:T(8,128)S(1)} fusion(f32[64,16]{0,1:T(8,128)S(1)} %broadcast_in_dim.53, s32[512]{0:T(512)S(1)} %bitcast.56, f32[512]{0:T(512)S(1)} %get-tuple-element.89), kind=kCustom, calls=%fused_computation.2 | custom fusion | bytes 10240 | tf_op jit(solution)/shard_map/scatter | solution.py:93
  32.4 0.0 copy-start.2
  32.4 0.3 copy.34
  32.7 0.1 broadcast_in_dim.48
  32.9 0.6 copy-done.2
  33.5 26.3 %scatter_fusion = f32[64,16,256]{2,1,0:T(8,128)S(1)} fusion(f32[64,16,256]{2,1,0:T(8,128)S(1)} %broadcast_in_dim.48, s32[512]{0:T(512)S(1)} %bitcast.57, f32[512,256]{1,0:T(8,128)S(1)} %copy-done.2), kind=kCustom, calls=%fused_computation.1 | custom fusion | bytes 1576960 | tf_op jit(solution)/shard_map/scatter | solution.py:88
  59.8 1.3 pad_maximum_fusion
  61.1 14.9 %all-to-all-start = ((f32[64,16,257]{2,1,0:T(8,128)}), f32[64,16,257]{2,1,0:T(8,128)S(1)}, u32[]{:S(2)}, u32[]{:S(2)}) async-start(f32[64,16,257]{2,1,0:T(8,128)} %pad_maximum_fusion), calls=%async_computation | async-start | bytes 3145728 | tf_op jit(solution)/shard_map/all_to_all | solution.py:45
  76.0 0.8 select_reduce_fusion
  76.8 0.9 concatenate.35
  77.7 1.0 fusion.10
  78.7 0.8 pad_maximum_fusion.2
  79.4 35.6 %all-to-all-done = f32[64,16,257]{2,1,0:T(8,128)S(1)} async-done(((f32[64,16,257]{2,1,0:T(8,128)}), f32[64,16,257]{2,1,0:T(8,128)S(1)}, u32[]{:S(2)}, u32[]{:S(2)}) %all-to-all-start) | async-done | bytes 1052704 | tf_op jit(solution)/shard_map/all_to_all | solution.py:45
  115.1 6.8 %all-to-all-start.2 = ((f32[8,32,257]{2,1,0:T(8,128)}), f32[8,32,257]{2,1,0:T(8,128)}, u32[]{:S(2)}, u32[]{:S(2)}) async-start(f32[8,32,257]{2,1,0:T(8,128)} %pad_maximum_fusion.2), calls=%async_computation.2 | async-start | bytes 786432 | tf_op jit(solution)/shard_map/all_to_all | solution.py:19
  121.9 1.2 fusion.12
  123.0 0.0 copy-done.1
  123.0 0.1 convert_element_type.21
  123.1 1.3 split.9
  124.4 5.0 %while.13 = (s32[]{:T(128)}, f32[1024,256]{1,0:T(8,128)S(1)}, f32[1024]{0:T(1024)S(1)}, s32[2,512]{1,0:T(2,128)S(1)}, f32[2,512,256]{2,1,0:T(8,128)S(1)}, /*index=5*/s32[]{:T(128)}, s32[]{:T(128)}) while((s32[]{:T(128)}, f32[1024,256]{1,0:T(8,128)S(1)}, f32[1024]{0:T(1024)S(1)}, s32[2,512]{1,0:T(2,128)S(1)}, ...), condition=%wide.region_8.9_spmd.clone, body=%wide.region_6.0_spmd.clone.sunk | while | flops 1613235200 | bytes 2646120 | solution.py:120
  124.5 0.3 fusion.37
  124.7 2.2 %fusion.36 = f32[1024,256]{1,0:T(8,128)S(1)} fusion(f32[1024,256]{1,0:T(8,128)S(1)} %get-tuple-element.129, s32[512]{0:T(512)S(1)} %bitcast.62, f32[2,512,256]{2,1,0:T(8,128)S(1)} %get-tuple-element.139, s32[]{:T(128)S(6)} %copy.46, pred[]{:T(512)S(6)} %compare.22), kind=kOutput, calls=%fused_computation.8.clone.1 | convolution fusion | flops 1611661312 | bytes 2623493 | tf_op jit(solution)/shard_map/while/body/eval_jaxpr/dot_general | solution.py:106
  126.9 0.3 fusion.37
  127.2 2.2 %fusion.36 = f32[1024,256]{1,0:T(8,128)S(1)} fusion(f32[1024,256]{1,0:T(8,128)S(1)} %get-tuple-element.129, s32[512]{0:T(512)S(1)} %bitcast.62, f32[2,512,256]{2,1,0:T(8,128)S(1)} %get-tuple-element.139, s32[]{:T(128)S(6)} %copy.46, pred[]{:T(512)S(6)} %compare.22), kind=kOutput, calls=%fused_computation.8.clone.1 | convolution fusion | flops 1611661312 | bytes 2623493 | tf_op jit(solution)/shard_map/while/body/eval_jaxpr/dot_general | solution.py:106
  129.4 0.2 copy.35
  129.6 0.1 pad_maximum_fusion.1
  129.8 1.5 copy.36
  131.2 3.3 %all-to-all-done.2 = f32[8,32,257]{2,1,0:T(8,128)} async-done(((f32[8,32,257]{2,1,0:T(8,128)}), f32[8,32,257]{2,1,0:T(8,128)}, u32[]{:S(2)}, u32[]{:S(2)}) %all-to-all-start.2) | async-done | bytes 263200 | tf_op jit(solution)/shard_map/all_to_all | solution.py:19
  134.5 3.6 %all-to-all-start.1 = ((f32[8,128,257]{1,2,0:T(8,128)}), f32[8,128,257]{1,2,0:T(8,128)S(1)}, u32[]{:S(2)}, u32[]{:S(2)}) async-start(f32[8,128,257]{1,2,0:T(8,128)} %copy.36), calls=%async_computation.1 | async-start | bytes 2162688 | tf_op jit(solution)/shard_map/all_to_all | solution.py:19
  138.1 1.0 reduce_sum.48
  139.1 0.1 slice_reduce_fusion.1
  139.2 26.8 %all-reduce = (f32[32,256]{1,0:T(8,128)S(1)}, f32[32]{0:T(128)S(1)}) all-reduce(f32[32,256]{1,0:T(8,128)S(1)} %slice.33, f32[32]{0:T(128)S(1)} %slice_reduce_fusion.1), channel_id=1, replica_groups=mesh['owner_0'=8,'owner_1'=4,'owner_2'=2,'rep'=8] {'owner_0'}, use_global_device_ids=true, to_apply=%region_12.13 | all-reduce | flops 8224 | bytes 65792 | tf_op jit(solution)/shard_map/psum | solution.py:36
  166.0 11.9 %all-reduce.1 = (f32[32,256]{1,0:T(8,128)S(1)}, f32[32]{0:T(128)S(1)}) all-reduce(f32[32,256]{1,0:T(8,128)S(1)} %get-tuple-element.77, f32[32]{0:T(128)S(1)} %get-tuple-element.78), channel_id=1, replica_groups=mesh['owner_0'=8,'owner_1'=4,'owner_2'=2,'rep'=8] {'owner_1'}, use_global_device_ids=true, to_apply=%region_13.14 | all-reduce | flops 8224 | bytes 65792 | tf_op jit(solution)/shard_map/psum | solution.py:36
  177.9 13.6 %all-reduce.2 = (f32[32,256]{1,0:T(8,128)S(1)}, f32[32]{0:T(128)S(1)}) all-reduce(f32[32,256]{1,0:T(8,128)S(1)} %get-tuple-element.79, f32[32]{0:T(128)S(1)} %get-tuple-element.80), channel_id=1, replica_groups=mesh['owner_0'=8,'owner_1'=4,'owner_2'=2,'rep'=8] {'owner_2'}, use_global_device_ids=true, to_apply=%region_14.15 | all-reduce | flops 8224 | bytes 65792 | tf_op jit(solution)/shard_map/psum | solution.py:36
  191.4 0.0 copy-start.6
  191.5 0.7 broadcast_divide_fusion
  192.2 0.0 all-to-all-done.1
  192.2 0.1 reduce_sum.46
  192.2 0.5 slice_bitcast_fusion
  192.8 0.8 copy.38
  (25 shorter events, 0.2 us)
Async XLA Ops:
  0.6 1.7 copy-start
  0.6 4.9 %copy-start.5 = (s32[512]{0:T(512)S(1)}, s32[512]{0:T(512)}, u32[]{:S(2)}) copy-start(s32[512]{0:T(512)} %param.9) | copy-start | bytes 6148
  32.4 1.0 copy-start.2
  61.1 14.9 %copy-start.3 = (s32[512]{0:T(512)S(1)}, s32[512]{0:T(512)}, u32[]{:S(2)}) copy-start(s32[512]{0:T(512)} %param.8) | copy-start | bytes 6148
  61.1 15.0 %copy-start.4 = (s32[256]{0:T(256)S(1)}, s32[256]{0:T(256)}, u32[]{:S(2)}) copy-start(s32[256]{0:T(256)} %param.11) | copy-start | bytes 3076
  61.1 54.0 %all-to-all-start = ((f32[64,16,257]{2,1,0:T(8,128)}), f32[64,16,257]{2,1,0:T(8,128)S(1)}, u32[]{:S(2)}, u32[]{:S(2)}) async-start(f32[64,16,257]{2,1,0:T(8,128)} %pad_maximum_fusion), calls=%async_computation | async-start | bytes 3145728 | tf_op jit(solution)/shard_map/all_to_all | solution.py:45
  115.1 8.0 %copy-start.1 = (f32[64,16,257]{2,1,0:T(8,128)}, f32[64,16,257]{2,1,0:T(8,128)S(1)}, u32[]{:S(2)}) copy-start(f32[64,16,257]{2,1,0:T(8,128)S(1)} %all-to-all-done) | copy-start | bytes 3158020
  115.1 19.4 %all-to-all-start.2 = ((f32[8,32,257]{2,1,0:T(8,128)}), f32[8,32,257]{2,1,0:T(8,128)}, u32[]{:S(2)}, u32[]{:S(2)}) async-start(f32[8,32,257]{2,1,0:T(8,128)} %pad_maximum_fusion.2), calls=%async_computation.2 | async-start | bytes 786432 | tf_op jit(solution)/shard_map/all_to_all | solution.py:19
  134.5 57.7 %all-to-all-start.1 = ((f32[8,128,257]{1,2,0:T(8,128)}), f32[8,128,257]{1,2,0:T(8,128)S(1)}, u32[]{:S(2)}, u32[]{:S(2)}) async-start(f32[8,128,257]{1,2,0:T(8,128)} %copy.36), calls=%async_computation.1 | async-start | bytes 2162688 | tf_op jit(solution)/shard_map/all_to_all | solution.py:19
  191.4 2.1 %copy-start.6 = (f32[32]{0:T(128)}, f32[32]{0:T(128)S(1)}, u32[]{:S(2)}) copy-start(f32[32]{0:T(128)S(1)} %get-tuple-element.82) | copy-start | bytes 388
where the time goes:
time: 194 us
  local copies, waits for them, and re-layouts  60.8 us (31%)
  blocking collectives  52.2 us (27%)
  waiting for transfers between devices  38.9 us (20%)
  starting transfers between devices  25.3 us (13%)
  other arithmetic  10.1 us (5%)
  matrix products  5.27 us (3%)
    psum x3, blocking collectives, one_axis_at_a_time(): shard = lax.psum(shard, axis)  52.2 us
    all_to_all x1, waiting for transfers between devices, sent_together(): lax.all_to_all(both, axis, split_axis=split_dim, concat_axis=concat_dim,...  35.6 us
    scatter x1, local copies, waits for them, and re-layouts, local(): bucket = jnp.zeros((owners, capacity, width), jnp.float32).at[target_safe...  26.3 us
    scatter x1, local copies, waits for them, and re-layouts, local(): labels = jnp.full((owners, capacity), -1.0, jnp.float32).at[target_safe,...  25.2 us
    all_to_all x1, starting transfers between devices, sent_together(): lax.all_to_all(both, axis, split_axis=split_dim, concat_axis=concat_dim,...  14.9 us
    all_to_all x2, starting transfers between devices, sent_and_summed(): lax.all_to_all(split_up(shard, dim, devices), axis, 0, 0, tiled=True)  10.4 us
    dot_general x2, matrix products, add_block(): lax.dot_general(onehot, block_rows, (((0,), (0,)), ((), ())), precision=l...  4.31 us
  transfers between devices with their start and end apart: 3, of which 2 were waited for; matrix products, arithmetic and copies ran while one was open for 7% of the time, Pallas kernels for 0%

commit v1 on v0

--- a/solution.py
+++ b/solution.py
@@ -33,7 +33,11 @@
 
 def one_axis_at_a_time(shard, axes):
     for axis in axes:
-        shard = lax.psum(shard, axis)
+
+        def end_the_frames(own_rows):
+            return jnp.sum(jax.lax.all_gather(own_rows, axis_name=axis), axis=0)
+
+        shard = end_the_frames(shard)
     return shard
 
 

time: 194 us -> 219 us (1.13)
  blocking collectives: 52.2 us -> 69.7 us
  local copies, waits for them, and re-layouts: 60.8 us -> 65.6 us
    psum x3 -> x0, blocking collectives: 52.2 us -> none  [one_axis_at_a_time(): shard = lax.psum(shard, axis)]
    all_gather x0 -> x3, blocking collectives: none -> 38.6 us  [end_the_frames(): return jnp.sum(jax.lax.all_gather(own_rows, axis_name=axis), axis=0)]
    unnamed x0 -> x3, blocking collectives: none -> 31.1 us
    unnamed x15 -> x24, local copies, waits for them, and re-layouts: 1.38 us -> 5.91 us
  transfers between devices with their start and end apart: 3 -> 3, of which waited for: 2 -> 2; matrix products, arithmetic and copies ran while one was open for 7% -> 9% of each run, Pallas kernels for 0% -> 0%
where the time goes in v1:
time: 219 us; the launch traced here: 218 us
  blocking collectives  69.7 us (32%)
  local copies, waits for them, and re-layouts  65.6 us (30%)
  waiting for transfers between devices  38.9 us (18%)
  starting transfers between devices  25.3 us (12%)
  other arithmetic  10.2 us (5%)
  matrix products  5.26 us (2%)
  between operations  2.86 us (1%)
    all_gather x3, blocking collectives, end_the_frames(): return jnp.sum(jax.lax.all_gather(own_rows, axis_name=axis), axis=0)  38.6 us
    all_to_all x1, waiting for transfers between devices, sent_together(): lax.all_to_all(both, axis, split_axis=split_dim, concat_axis=concat_dim,...  35.6 us
    unnamed x3, blocking collectives  31.1 us
    scatter x1, local copies, waits for them, and re-layouts, local(): bucket = jnp.zeros((owners, capacity, width), jnp.float32).at[target_safe...  26.3 us
    scatter x1, local copies, waits for them, and re-layouts, local(): labels = jnp.full((owners, capacity), -1.0, jnp.float32).at[target_safe,...  25.2 us
    all_to_all x1, starting transfers between devices, sent_together(): lax.all_to_all(both, axis, split_axis=split_dim, concat_axis=concat_dim,...  14.9 us
    all_to_all x2, starting transfers between devices, sent_and_summed(): lax.all_to_all(split_up(shard, dim, devices), axis, 0, 0, tiled=True)  10.4 us
    unnamed x24, local copies, waits for them, and re-layouts  5.91 us
  transfers between devices with their start and end apart: 3, of which 2 were waited for; matrix products, arithmetic and copies ran while one was open for 9% of the time, Pallas kernels for 0%

profile of v1, /device:TPU:1, one launch (start us, length us, event | category | flops | bytes accessed | tf_op | source)
XLA Modules:
  0.0 217.9 jit_solution(9582196979197142040)
XLA Ops:
  0.7 0.7 compare_select_fusion.2
  1.4 0.9 compare_reduce_fusion
  2.3 3.1 %gather_fusion = s32[512]{0:T(512)S(1)} fusion(s32[65536]{0:T(1024)S(1)} %copy-done, s32[1024]{0:T(1024)S(1)} %pad_clamp_fusion), kind=kCustom, calls=%fused_computation | custom fusion | bytes 6144 | tf_op jit(solution)/shard_map/gather | solution.py:79
  5.6 1.2 reduce-window.6
  6.8 0.2 slice_reduce_fusion
  7.0 0.1 fusion.19
  7.2 25.2 %scatter_fusion.1 = f32[64,16]{0,1:T(8,128)S(1)} fusion(f32[64,16]{0,1:T(8,128)S(1)} %broadcast_in_dim.53, s32[512]{0:T(512)S(1)} %bitcast.60, f32[512]{0:T(512)S(1)} %get-tuple-element.83), kind=kCustom, calls=%fused_computation.2 | custom fusion | bytes 10240 | tf_op jit(solution)/shard_map/scatter | solution.py:97
  32.4 0.3 copy.34
  32.7 0.1 broadcast_in_dim.48
  32.9 0.6 copy-done.2
  33.4 26.3 %scatter_fusion = f32[64,16,256]{2,1,0:T(8,128)S(1)} fusion(f32[64,16,256]{2,1,0:T(8,128)S(1)} %broadcast_in_dim.48, s32[512]{0:T(512)S(1)} %bitcast.61, f32[512,256]{1,0:T(8,128)S(1)} %copy-done.2), kind=kCustom, calls=%fused_computation.1 | custom fusion | bytes 1576960 | tf_op jit(solution)/shard_map/scatter | solution.py:92
  59.8 1.3 pad_maximum_fusion
  61.1 14.9 %all-to-all-start = ((f32[64,16,257]{2,1,0:T(8,128)}), f32[64,16,257]{2,1,0:T(8,128)S(1)}, u32[]{:S(2)}, u32[]{:S(2)}) async-start(f32[64,16,257]{2,1,0:T(8,128)} %pad_maximum_fusion), calls=%async_computation | async-start | bytes 3145728 | tf_op jit(solution)/shard_map/all_to_all | solution.py:49
  76.0 0.8 select_reduce_fusion
  76.8 0.9 concatenate.35
  77.7 1.0 fusion.10
  78.7 0.8 pad_maximum_fusion.2
  79.4 35.6 %all-to-all-done = f32[64,16,257]{2,1,0:T(8,128)S(1)} async-done(((f32[64,16,257]{2,1,0:T(8,128)}), f32[64,16,257]{2,1,0:T(8,128)S(1)}, u32[]{:S(2)}, u32[]{:S(2)}) %all-to-all-start) | async-done | bytes 1052704 | tf_op jit(solution)/shard_map/all_to_all | solution.py:49
  115.1 6.8 %all-to-all-start.2 = ((f32[8,32,257]{2,1,0:T(8,128)}), f32[8,32,257]{2,1,0:T(8,128)}, u32[]{:S(2)}, u32[]{:S(2)}) async-start(f32[8,32,257]{2,1,0:T(8,128)} %pad_maximum_fusion.2), calls=%async_computation.2 | async-start | bytes 786432 | tf_op jit(solution)/shard_map/all_to_all | solution.py:19
  121.9 1.2 fusion.12
  123.1 1.3 split.9
  124.4 5.0 %while.13 = (s32[]{:T(128)}, f32[1024,256]{1,0:T(8,128)S(1)}, f32[1024]{0:T(1024)S(1)}, s32[2,512]{1,0:T(2,128)S(1)}, f32[2,512,256]{2,1,0:T(8,128)S(1)}, /*index=5*/s32[]{:T(128)}, s32[]{:T(128)}) while((s32[]{:T(128)}, f32[1024,256]{1,0:T(8,128)S(1)}, f32[1024]{0:T(1024)S(1)}, s32[2,512]{1,0:T(2,128)S(1)}, ...), condition=%wide.region_8.9_spmd.clone, body=%wide.region_6.0_spmd.clone.sunk | while | flops 1613235200 | bytes 2646112 | solution.py:124
  124.4 2.1 fusion.36
  126.6 0.3 fusion.37
  126.9 2.2 fusion.36
  129.1 0.3 fusion.37
  129.4 0.2 copy.35
  129.6 0.1 pad_maximum_fusion.1
  129.8 1.5 copy.36
  131.2 3.3 %all-to-all-done.2 = f32[8,32,257]{2,1,0:T(8,128)} async-done(((f32[8,32,257]{2,1,0:T(8,128)}), f32[8,32,257]{2,1,0:T(8,128)}, u32[]{:S(2)}, u32[]{:S(2)}) %all-to-all-start.2) | async-done | bytes 263200 | tf_op jit(solution)/shard_map/all_to_all | solution.py:19
  134.5 3.6 %all-to-all-start.1 = ((f32[8,128,257]{1,2,0:T(8,128)}), f32[8,128,257]{1,2,0:T(8,128)S(1)}, u32[]{:S(2)}, u32[]{:S(2)}) async-start(f32[8,128,257]{1,2,0:T(8,128)} %copy.36), calls=%async_computation.1 | async-start | bytes 2162688 | tf_op jit(solution)/shard_map/all_to_all | solution.py:19
  138.1 1.3 dynamic-slice
  139.3 1.3 dynamic-slice.1
  141.9 1.3 dynamic-slice.2
  143.8 1.0 reduce_sum.102
  144.9 0.1 slice_reduce_fusion.1
  145.0 0.2 dynamic-update-slice
  145.2 16.1 %all-reduce = f32[256]{0:T(256)S(1)} all-reduce(f32[256]{0:T(256)S(1)} %dynamic-update-slice), channel_id=5, replica_groups=mesh['owner_0'=8,'owner_1'=4,'owner_2'=2,'rep'=8] {'owner_0'}, use_global_device_ids=true, to_apply=%add | all-reduce | flops 256 | bytes 2048
  161.4 0.2 dynamic-update-slice.1
  161.6 7.0 %all-reduce.1 = f32[128]{0:T(128)S(1)} all-reduce(f32[128]{0:T(128)S(1)} %dynamic-update-slice.1), channel_id=6, replica_groups=mesh['owner_0'=8,'owner_1'=4,'owner_2'=2,'rep'=8] {'owner_1'}, use_global_device_ids=true, to_apply=%add.1 | all-reduce | flops 128 | bytes 1024
  168.7 0.2 dynamic-update-slice.2
  169.0 8.0 %all-reduce.2 = f32[64]{0:T(128)S(1)} all-reduce(f32[64]{0:T(128)S(1)} %dynamic-update-slice.2), channel_id=7, replica_groups=mesh['owner_0'=8,'owner_1'=4,'owner_2'=2,'rep'=8] {'owner_2'}, use_global_device_ids=true, to_apply=%add.2 | all-reduce | flops 64 | bytes 512
  177.1 18.4 %all-gather = f32[256,256]{1,0:T(8,128)S(1)} all-gather(f32[32,256]{1,0:T(8,128)S(1)} %slice.33), channel_id=2, replica_groups=mesh['owner_0'=8,'owner_1'=4,'owner_2'=2,'rep'=8] {'owner_0'}, dimensions={0}, use_global_device_ids=true | all-gather | bytes 294912 | tf_op jit(solution)/shard_map/all_gather | solution.py:38
  195.6 9.1 %all-gather.1 = f32[128,256]{1,0:T(8,128)S(1)} all-gather(f32[32,256]{1,0:T(8,128)S(1)} %reduce_sum.103), channel_id=3, replica_groups=mesh['owner_0'=8,'owner_1'=4,'owner_2'=2,'rep'=8] {'owner_1'}, dimensions={0}, use_global_device_ids=true | all-gather | bytes 163840 | tf_op jit(solution)/shard_map/all_gather | solution.py:38
  204.7 11.1 %all-gather.2 = f32[64,256]{1,0:T(8,128)S(1)} all-gather(f32[32,256]{1,0:T(8,128)S(1)} %reduce_sum.104), channel_id=4, replica_groups=mesh['owner_0'=8,'owner_1'=4,'owner_2'=2,'rep'=8] {'owner_2'}, dimensions={0}, use_global_device_ids=true | all-gather | bytes 98304 | tf_op jit(solution)/shard_map/all_gather | solution.py:38
  215.8 0.7 broadcast_divide_fusion
  216.6 0.5 slice_bitcast_fusion
  217.1 0.8 copy.38
  (46 shorter events, 0.7 us)
Async XLA Ops:
  0.6 1.7 copy-start
  0.6 4.9 %copy-start.5 = (s32[512]{0:T(512)S(1)}, s32[512]{0:T(512)}, u32[]{:S(2)}) copy-start(s32[512]{0:T(512)} %param.9) | copy-start | bytes 6148
  32.4 1.0 copy-start.2
  61.1 14.9 %copy-start.3 = (s32[512]{0:T(512)S(1)}, s32[512]{0:T(512)}, u32[]{:S(2)}) copy-start(s32[512]{0:T(512)} %param.8) | copy-start | bytes 6148
  61.1 15.0 %copy-start.4 = (s32[256]{0:T(256)S(1)}, s32[256]{0:T(256)}, u32[]{:S(2)}) copy-start(s32[256]{0:T(256)} %param.11) | copy-start | bytes 3076
  61.1 54.0 %all-to-all-start = ((f32[64,16,257]{2,1,0:T(8,128)}), f32[64,16,257]{2,1,0:T(8,128)S(1)}, u32[]{:S(2)}, u32[]{:S(2)}) async-start(f32[64,16,257]{2,1,0:T(8,128)} %pad_maximum_fusion), calls=%async_computation | async-start | bytes 3145728 | tf_op jit(solution)/shard_map/all_to_all | solution.py:49
  115.1 8.0 %copy-start.1 = (f32[64,16,257]{2,1,0:T(8,128)}, f32[64,16,257]{2,1,0:T(8,128)S(1)}, u32[]{:S(2)}) copy-start(f32[64,16,257]{2,1,0:T(8,128)S(1)} %all-to-all-done) | copy-start | bytes 3158020
  115.1 19.4 %all-to-all-start.2 = ((f32[8,32,257]{2,1,0:T(8,128)}), f32[8,32,257]{2,1,0:T(8,128)}, u32[]{:S(2)}, u32[]{:S(2)}) async-start(f32[8,32,257]{2,1,0:T(8,128)} %pad_maximum_fusion.2), calls=%async_computation.2 | async-start | bytes 786432 | tf_op jit(solution)/shard_map/all_to_all | solution.py:19
  134.5 82.0 %all-to-all-start.1 = ((f32[8,128,257]{1,2,0:T(8,128)}), f32[8,128,257]{1,2,0:T(8,128)S(1)}, u32[]{:S(2)}, u32[]{:S(2)}) async-start(f32[8,128,257]{1,2,0:T(8,128)} %copy.36), calls=%async_computation.1 | async-start | bytes 2162688 | tf_op jit(solution)/shard_map/all_to_all | solution.py:19
  177.1 40.8 %copy-start.6 = (f32[32]{0:T(128)}, f32[32]{0:T(128)S(1)}, u32[]{:S(2)}) copy-start(f32[32]{0:T(128)S(1)} %reduce_sum.108) | copy-start | bytes 388
